TPU v7x, 256 devices: a whole 4x4x8 slice. The times are simulated.
256 devices in a mesh: vocab: 32 (over z, y), batch: 8 (over x, core).
Axes of the slice: x: 4, y: 4, z: 8, core: 2. Of those that a mesh axis runs over, the one named last changes fastest.
Arguments:
- latent_state_rows: bfloat16 [128, 8192], P('batch', 'vocab'), may hold values from -90 to 90
- closing_rescale_coeffs: bfloat16 [8192], replicated, may hold values from 0.5 to 1.5
- output_projection_matrix: bfloat16 [8192, 131072], P(None, ('vocab', 'batch')), may hold values from -3.7565048 to 3.7565048
- config_heat_values: float32 [16], replicated, may hold values from 0.7 to 1.4
- sequence_config_choice: int32 [128], replicated, may hold values from 0 to 15
- ranked_choice_ids: int32 [128, 128], replicated, may hold values from 0 to 131071
- keep_count: int32 [128], replicated, may hold values from 2 to 128
Outputs:
- log_norm: float32 [128], P('batch')
- kept_mass: float32 [128], P('batch')
- renormed: float32 [128, 128], P('batch')
All inputs are finite; a program needn't handle non-finite values.
Results may differ from a plain program's by a relative error of at most 0.0048.
Values may be sent and summed in bfloat16 or wider, within the bound.
A program may use at most 64 MiB of HBM per device.

v0:
```python
import jax
import jax.numpy as jnp
from jax import lax
from jax.sharding import Mesh
from jax.sharding import PartitionSpec as P

VOCAB = ("vocab_0", "vocab_1")
VOCAB_BATCH = ("vocab_0", "vocab_1", "batch")


epsilon = 1e-06


def gather_axes(value, axes, dim):
    whole = value
    for number in range(len(axes) - 1, -1, -1):
        whole = lax.all_gather(whole, axes[number], axis=dim, tiled=True)
    return whole


def from_everyone(value, axis):
    copies = jnp.broadcast_to(value, (lax.axis_size(axis), *value.shape))
    return lax.all_to_all(copies, axis, split_axis=0, concat_axis=0, tiled=True)


def in_order(blocks, dim):
    blocks = jnp.moveaxis(blocks, 0, dim)
    shape = blocks.shape
    return blocks.reshape(*shape[:dim], shape[dim] * shape[dim + 1], *shape[dim + 2 :])


def gather_directly(value, axis, dim):
    blocks = from_everyone(value, axis)
    return in_order(blocks, dim)


def side_by_side(arrays, axis, split_dim, concat_dim, along):
    both = jnp.concatenate(arrays, axis=along)
    whole, at, gathered = (
        lax.all_to_all(both, axis, split_axis=split_dim, concat_axis=concat_dim, tiled=True),
        0,
        [],
    )
    for a in arrays:
        gathered.append(lax.slice_in_dim(whole, at, at + a.shape[along], axis=along))
        at += a.shape[along]
    return tuple(gathered)


def all_in_one(value, axis):
    leaves = jax.tree.leaves(value)
    turns = sorted(range(len(leaves)), key=lambda k: -leaves[k].size)
    width = (1, *leaves[turns[0]].shape)[-1]
    lines = [
        jnp.pad(leaves[k].reshape(-1), (0, -leaves[k].size % width)).reshape(-1, width)
        for k in turns
    ]
    both, at, found = (from_everyone(jnp.concatenate(lines), axis), 0, {})
    for k, line in zip(turns, lines):
        piece = both[:, at : at + len(line)].reshape(len(both), -1)
        found[k] = piece[:, : leaves[k].size].reshape(-1, *leaves[k].shape)
        at += len(line)
    numbers = iter(range(len(leaves)))
    return jax.tree.map(lambda _: found[next(numbers)], value)


def joined_by_halves(pieces, combine):
    while len(jax.tree.leaves(pieces)[0]) > 1:
        pieces = jax.vmap(combine)(
            *(jax.tree.map(lambda part: part[side::2], pieces) for side in (0, 1))
        )
    return jax.tree.map(lambda part: part[0], pieces)


def merged(value, axis, combine):
    pieces = all_in_one(value, axis)
    return joined_by_halves(pieces, combine)


def normalize(values, gain_part, mean_square):
    factor = lax.rsqrt(mean_square + epsilon)
    return (values * factor[:, None] * gain_part[None, :]).astype(jnp.bfloat16)


def rows_normed(raw_rows, gain_full):
    values = raw_rows.astype(jnp.float32)
    return normalize(values, gain_full, jnp.mean(values * values, axis=1))


def merge_parts(earlier, later):
    top_first, total_first, cand_first = earlier
    top_second, total_second, cand_second = later
    row_top = jnp.maximum(top_first, top_second)
    row_total = total_first * jnp.exp(top_first - row_top) + total_second * jnp.exp(
        top_second - row_top
    )
    return (row_top, row_total, cand_first + cand_second)


def local(
    latent_state_rows,
    closing_rescale_coeffs,
    output_projection_matrix,
    config_heat_values,
    sequence_config_choice,
    ranked_choice_ids,
    keep_count,
):
    group_rows = latent_state_rows.shape[0]
    col_count = output_projection_matrix.shape[1]
    batch_count = lax.axis_size("batch")
    vocab_pos = lax.axis_index(VOCAB)
    batch_pos = lax.axis_index("batch")
    gain_full = closing_rescale_coeffs.astype(jnp.float32)
    wide_rows = gather_axes(latent_state_rows, VOCAB, 1)
    unnormalized_scores = jnp.dot(
        rows_normed(gather_directly(wide_rows, "batch", 0), gain_full),
        output_projection_matrix,
        preferred_element_type=jnp.float32,
    )
    config_membership = (
        sequence_config_choice[:, None]
        == jnp.arange(config_heat_values.shape[0], dtype=jnp.int32)[None, :]
    ).astype(jnp.float32)
    sequence_heat_values = jnp.sum(config_membership * config_heat_values[None, :], axis=1)
    divided_scores = unnormalized_scores / sequence_heat_values[:, None]
    offset = (vocab_pos * batch_count + batch_pos) * col_count
    local_ids = ranked_choice_ids - offset
    owned = (local_ids >= 0) & (local_ids < col_count)
    picked = jnp.take_along_axis(divided_scores, jnp.clip(local_ids, 0, col_count - 1), axis=1)
    cand_local = jnp.where(owned, picked, jnp.float32(0.0))
    local_top = jnp.max(divided_scores, axis=1)
    first_slot = batch_pos * group_rows
    local_total = jnp.sum(jnp.exp(divided_scores - local_top[:, None]), axis=1)
    slot_count = local_top.shape[0]
    tops_in, totals_in, cands_in = side_by_side(
        (
            local_top.reshape(slot_count, 1, 1),
            local_total.reshape(slot_count, 1, 1),
            cand_local.reshape(slot_count, 1, cand_local.shape[1]),
        ),
        "batch",
        0,
        1,
        2,
    )
    group_top = jnp.max(tops_in[:, :, 0], axis=1)
    group_total = jnp.sum(
        totals_in[:, :, 0] * jnp.exp(tops_in[:, :, 0] - group_top[:, None]), axis=1
    )
    group_cand = jnp.sum(cands_in, axis=1)
    own_top, own_total, own_cand = merged((group_top, group_total, group_cand), VOCAB, merge_parts)
    own_cutoff = lax.dynamic_slice_in_dim(keep_count, first_slot, group_rows)
    log_norm = own_top + jnp.log(own_total)
    kept_mask = jnp.arange(own_cand.shape[1], dtype=jnp.int32)[None, :] < own_cutoff[:, None]
    kept_top = jnp.max(jnp.where(kept_mask, own_cand, jnp.float32(-3e38)), axis=1)
    shifted = jnp.where(kept_mask, own_cand - kept_top[:, None], jnp.float32(0.0))
    kept_exp = jnp.where(kept_mask, jnp.exp(shifted), jnp.float32(0.0))
    kept_sum = jnp.sum(kept_exp, axis=1)
    kept_mass = kept_top + jnp.log(kept_sum) - log_norm
    return (log_norm, kept_mass, kept_exp / kept_sum[:, None])


def solution(mesh):
    torus = Mesh(mesh.devices.reshape(8, 4, mesh.shape["batch"]), ("vocab_0", "vocab_1", "batch"))
    in_specs = (P("batch", VOCAB), P(), P(None, VOCAB_BATCH), P(), P(), P(), P())
    out_specs = (P("batch"), P("batch"), P("batch", None))
    return jax.shard_map(local, mesh=torus, in_specs=in_specs, out_specs=out_specs, check_vma=False)
```

profile of v0, /device:TPU:1, one launch (start us, length us, event | category | flops | bytes accessed | tf_op | source)
XLA Modules:
  0.0 244.5 jit_solution(13653594398315137193)
XLA Ops:
  0.6 10.6 %all_gather.6 = bf16[16,1024]{1,0:T(8,128)(2,1)S(1)} all-gather(bf16[16,256]{1,0:T(8,128)(2,1)} %param.7), channel_id=1, replica_groups=mesh['vocab_0'=8,'vocab_1'=4,'batch'=8] {'vocab_1'}, dimensions={1}, use_global_device_ids=true | all-gather | bytes 40960 | tf_op jit(solution)/shard_map/all_gather | solution.py:17
  11.2 22.0 %all_gather.7 = bf16[16,8192]{1,0:T(8,128)(2,1)S(1)} all-gather(bf16[16,1024]{1,0:T(8,128)(2,1)S(1)} %all_gather.6), channel_id=1, replica_groups=mesh['vocab_0'=8,'vocab_1'=4,'batch'=8] {'vocab_0'}, dimensions={1}, use_global_device_ids=true | all-gather | bytes 294912 | tf_op jit(solution)/shard_map/all_gather | solution.py:17
  33.3 1.6 broadcast_in_dim.34
  34.8 14.2 %all-to-all-start = ((bf16[8,16,8192]{2,1,0:T(8,128)(2,1)}), bf16[8,16,8192]{2,1,0:T(8,128)(2,1)S(1)}, u32[]{:S(2)}, u32[]{:S(2)}) async-start(bf16[8,16,8192]{2,1,0:T(8,128)(2,1)} %broadcast_in_dim.34), calls=%async_computation | async-start | bytes 4194304 | tf_op jit(solution)/shard_map/all_to_all | solution.py:23
  49.0 0.7 convert_element_type.22
  49.8 0.8 select_reduce_fusion.1
  50.5 0.9 fusion.3
  51.4 23.8 %all-to-all-done = bf16[8,16,8192]{2,1,0:T(8,128)(2,1)S(1)} async-done(((bf16[8,16,8192]{2,1,0:T(8,128)(2,1)}), bf16[8,16,8192]{2,1,0:T(8,128)(2,1)S(1)}, u32[]{:S(2)}, u32[]{:S(2)}) %all-to-all-start) | async-done | bytes 2097184 | tf_op jit(solution)/shard_map/all_to_all | solution.py:23
  75.2 0.5 multiply_reduce_fusion
  75.7 0.1 rsqrt.11
  75.8 0.7 fusion.1
  76.5 4.8 %fusion.10 = (f32[128]{0:T(128)S(1)}, f32[128,512]{1,0:T(8,128)S(1)}) fusion(f32[128]{0:T(128)S(1)} %select_reduce_fusion.1, bf16[128,8192]{1,0:T(8,128)(2,1)S(1)} %fusion.1, bf16[8192,512]{1,0:T(8,128)(2,1)} %param.9), kind=kOutput, calls=%fused_computation.45 | convolution fusion | flops 1073872768 | bytes 10748928 | tf_op jit(solution)/shard_map/dot_general | solution.py:116
  81.4 0.0 copy-start
  81.4 0.0 copy-start.1
  81.4 129.5 %gather_fusion = f32[16384]{0:T(1024)S(1)} fusion(f32[128,512]{1,0:T(8,128)S(1)} %get-tuple-element.19, s32[16384]{0:T(1024)S(1)} %fusion.3), kind=kCustom, calls=%fused_computation | custom fusion | bytes 262144 | tf_op jit(solution)/shard_map/jit(take_along_axis)/gather | solution.py:130
  210.9 0.0 copy-done
  210.9 0.2 exponential_reduce_fusion
  211.1 0.1 copy.24
  211.2 0.1 copy.23
  211.3 0.6 pad_maximum_fusion
  212.0 8.6 %all_to_all.28 = f32[128,1,130]{2,1,0:T(1,128)S(1)} all-to-all(f32[128,1,130]{2,1,0:T(1,128)S(1)} %pad_maximum_fusion), channel_id=1, replica_groups=mesh['vocab_0'=8,'vocab_1'=4,'batch'=8] {'batch'}, dimensions={0} | all-to-all | bytes 133120 | tf_op jit(solution)/shard_map/all_to_all | solution.py:40
  220.6 0.2 slice_reduce_fusion.3
  220.7 0.1 slice_reduce_fusion.1
  220.9 0.8 broadcast_in_dim.37
  221.6 6.9 %all-to-all-start.2 = ((f32[32,18,128]{2,1,0:T(8,128)}), f32[32,18,128]{2,1,0:T(8,128)S(1)}, u32[]{:S(2)}, u32[]{:S(2)}) async-start(f32[32,18,128]{2,1,0:T(8,128)} %broadcast_in_dim.37), calls=%async_computation.2 | async-start | bytes 786432 | tf_op jit(solution)/shard_map/all_to_all | solution.py:23
  228.5 0.0 copy-done.1
  228.5 0.1 dynamic_slice.3
  228.6 13.8 %all-to-all-done.2 = f32[32,18,128]{2,1,0:T(8,128)S(1)} async-done(((f32[32,18,128]{2,1,0:T(8,128)}), f32[32,18,128]{2,1,0:T(8,128)S(1)}, u32[]{:S(2)}, u32[]{:S(2)}) %all-to-all-start.2) | async-done | bytes 294944 | tf_op jit(solution)/shard_map/all_to_all | solution.py:23
  242.9 0.2 select_reduce_fusion
  243.1 0.2 fusion.6
  243.3 0.7 fusion.5
  244.0 0.5 add_subtract_fusion
  (32 shorter events, 0.5 us)
Async XLA Ops:
  34.8 40.4 %all-to-all-start = ((bf16[8,16,8192]{2,1,0:T(8,128)(2,1)}), bf16[8,16,8192]{2,1,0:T(8,128)(2,1)S(1)}, u32[]{:S(2)}, u32[]{:S(2)}) async-start(bf16[8,16,8192]{2,1,0:T(8,128)(2,1)} %broadcast_in_dim.34), calls=%async_computation | async-start | bytes 4194304 | tf_op jit(solution)/shard_map/all_to_all | solution.py:23
  81.4 129.5 %copy-start = (s32[128,128]{1,0:T(8,128)S(1)}, s32[128,128]{1,0:T(8,128)}, u32[]{:S(2)}) copy-start(s32[128,128]{1,0:T(8,128)} %param.12) | copy-start | bytes 196612
  81.4 147.2 %copy-start.1 = (s32[128]{0:T(128)S(1)}, s32[128]{0:T(128)}, u32[]{:S(2)}) copy-start(s32[128]{0:T(128)} %param.13) | copy-start | bytes 1540
  221.6 20.8 %all-to-all-start.2 = ((f32[32,18,128]{2,1,0:T(8,128)}), f32[32,18,128]{2,1,0:T(8,128)S(1)}, u32[]{:S(2)}, u32[]{:S(2)}) async-start(f32[32,18,128]{2,1,0:T(8,128)} %broadcast_in_dim.37), calls=%async_computation.2 | async-start | bytes 786432 | tf_op jit(solution)/shard_map/all_to_all | solution.py:23
where the time goes:
time: 245 us
  local copies, waits for them, and re-layouts  133 us (54%)
  blocking collectives  41.2 us (17%)
  waiting for transfers between devices  37.6 us (15%)
  starting transfers between devices  21.1 us (9%)
  other arithmetic  6.33 us (3%)
  matrix products  4.85 us (2%)
    gather x1, local copies, waits for them, and re-layouts, local(): jnp.take_along_axis(divided_scores, jnp.clip(local_ids, 0, col_count - 1)...  129 us
    all_to_all x2, waiting for transfers between devices, from_everyone(): return lax.all_to_all(copies, axis, split_axis=0, concat_axis=0, tiled=True)  37.6 us
    all_gather x2, blocking collectives, gather_axes(): whole = lax.all_gather(whole, axes[number], axis=dim, tiled=True)  32.6 us
    all_to_all x2, starting transfers between devices, from_everyone(): return lax.all_to_all(copies, axis, split_axis=0, concat_axis=0, tiled=True)  21.1 us
    all_to_all x1, blocking collectives, side_by_side(): lax.all_to_all(both, axis, split_axis=split_dim, concat_axis=concat_dim,...  8.59 us
  transfers between devices with their start and end apart: 2, of which 2 were waited for; matrix products, arithmetic and copies ran while one was open for 1% of the time, Pallas kernels for 0%

commit v1 on v0

v1 whole, which is shorter than its diff:
```python
import jax
import jax.numpy as jnp
from jax import lax
from jax.experimental import pallas as pl
from jax.experimental.pallas import tpu as pltpu
from jax.sharding import Mesh
from jax.sharding import PartitionSpec as P

NZ, NY, NX, NC = 8, 4, 4, 2
SG = 16
COLS = 512
LANES = 128
SLOTS = 128
D = 8192
EPS = 1e-06
MESH_ID = pl.DeviceIdType.MESH
ORDER = (0, 1, 7, 2, 6, 3, 5, 4)


def kernel(
    x_hbm, w_hbm, gain_hbm, ids_hbm, heat_ref, choice_hbm, keep_hbm,
    stat_out, ren_out,
    g_ref, w_ref, gain_ref, ids_ref, choice_ref, keep_ref,
    ssq_ref, acc_ref, m1_ref, r1_ref, r2_ref, r3_ref, m2_ref, m3_ref,
    in_sem, w_sem,
    s1_send, s1_recv, s2y_send, s2y_recv, s2x_send, s2x_recv,
    s3x_send, s3x_recv, s3y_send, s3y_recv,
    s4x_send, s4x_recv, s4y_send, s4y_recv, s5_send, s5_recv,
    q1_send, q1_recv, q2_send, q2_recv, q3_send, q3_recv,
):
    z0, y0, x0, c0 = (lax.axis_index(a) for a in ("z", "y", "x", "c"))

    def zp(k):
        return lax.rem(z0 + k, NZ)

    def yp(k):
        return lax.rem(y0 + k, NY)

    def xp(k):
        return lax.rem(x0 + k, NX)

    own = pltpu.make_async_copy(x_hbm, g_ref.at[z0, :, c0, x0, y0], in_sem.at[0])
    own.start()

    barrier = pltpu.get_barrier_semaphore()
    count = 0
    for k in range(1, NZ):
        pl.semaphore_signal(barrier, inc=1, device_id={"z": zp(k)}, device_id_type=MESH_ID)
        count += 1
    for k in range(1, NY):
        pl.semaphore_signal(barrier, inc=1, device_id={"y": yp(k)}, device_id_type=MESH_ID)
        count += 1
    for k in range(NX):
        for kc in range(NC):
            if k or kc:
                pl.semaphore_signal(
                    barrier, inc=1, device_id={"x": xp(k), "c": lax.rem(c0 + kc, NC)}, device_id_type=MESH_ID
                )
                count += 1

    w_copies = []
    for z in range(NZ):
        cp = pltpu.make_async_copy(w_hbm.at[z], w_ref.at[z], w_sem.at[z])
        cp.start()
        w_copies.append(cp)
    small = []
    for n, (src, dst) in enumerate(
        ((gain_hbm, gain_ref), (ids_hbm, ids_ref), (choice_hbm, choice_ref), (keep_hbm, keep_ref))
    ):
        cp = pltpu.make_async_copy(src, dst, in_sem.at[1 + n])
        cp.start()
        small.append(cp)
    own.wait()
    pl.semaphore_wait(barrier, count)

    sends = []

    def send(src, dst, ssem, rsem, to):
        cp = pltpu.make_async_remote_copy(
            src_ref=src, dst_ref=dst, send_sem=ssem, recv_sem=rsem, device_id=to, device_id_type=MESH_ID
        )
        cp.start()
        sends.append(cp)

    def landed(dst, ssem, rsem):
        pltpu.make_async_remote_copy(
            src_ref=dst, dst_ref=dst, send_sem=ssem, recv_sem=rsem, device_id={"z": z0}, device_id_type=MESH_ID
        ).wait_recv()

    for k in reversed(ORDER[1:]):
        blk = g_ref.at[z0, :, c0, x0, y0]
        send(blk, blk, s1_send.at[k], s1_recv.at[k], {"z": zp(k)})

    def stage2(k):
        z = zp(NZ - k)
        if k:
            landed(g_ref.at[z, :, c0, x0, y0], s1_send.at[k], s1_recv.at[k])
        for d in (2, 1, 3):
            a = g_ref.at[z, 0, c0, x0, y0]
            send(a, a, s2y_send.at[k, d], s2y_recv.at[k, d], {"y": yp(d)})
            b = g_ref.at[z, 1, c0, x0, y0]
            send(b, b, s2x_send.at[k, d], s2x_recv.at[k, d], {"x": xp(d)})

    def stage3(k):
        z = zp(NZ - k)
        for d in (1, 3, 2):
            landed(g_ref.at[z, 0, c0, x0, yp(NY - d)], s2y_send.at[k, d], s2y_recv.at[k, d])
        a = g_ref.at[z, 0, c0, x0]
        for d in (1, 3):
            send(a, a, s3x_send.at[k, d], s3x_recv.at[k, d], {"x": xp(d)})
        for d in (1, 3, 2):
            landed(g_ref.at[z, 1, c0, xp(NX - d), y0], s2x_send.at[k, d], s2x_recv.at[k, d])
        b = g_ref.at[z, 1, c0, :, y0]
        for d in (1, 3):
            send(b, b, s3y_send.at[k, d], s3y_recv.at[k, d], {"y": yp(d)})

    def stage4(k):
        z = zp(NZ - k)
        for d in (1, 3):
            part = pl.ds(0, 2) if d == 1 else pl.ds(2, 2)
            xs, ys = xp(NX - d), yp(NY - d)
            landed(g_ref.at[z, 0, c0, xs], s3x_send.at[k, d], s3x_recv.at[k, d])
            a = g_ref.at[z, 0, c0, xs, part]
            send(a, a, s4x_send.at[k, d], s4x_recv.at[k, d], {"x": xp(d)})
            landed(g_ref.at[z, 1, c0, :, ys], s3y_send.at[k, d], s3y_recv.at[k, d])
            b = g_ref.at[z, 1, c0, part, ys]
            send(b, b, s4y_send.at[k, d], s4y_recv.at[k, d], {"y": yp(d)})

    def stage5(k):
        z = zp(NZ - k)
        for d in (1, 3):
            part = pl.ds(0, 2) if d == 1 else pl.ds(2, 2)
            landed(g_ref.at[z, 0, c0, xp(2), part], s4x_send.at[k, d], s4x_recv.at[k, d])
            landed(g_ref.at[z, 1, c0, part, yp(2)], s4y_send.at[k, d], s4y_recv.at[k, d])
        blk = g_ref.at[z, :, c0]
        send(blk, blk, s5_send.at[k], s5_recv.at[k], {"c": lax.rem(c0 + 1, NC)})

    ssq_ref[...] = jnp.zeros_like(ssq_ref)

    def stage6(k):
        z = zp(NZ - k)
        landed(g_ref.at[z, :, lax.rem(c0 + 1, NC)], s5_send.at[k], s5_recv.at[k])
        total = ssq_ref[...]
        for h in range(2):
            for y in range(NY):
                v = g_ref[z, h, :, :, y].reshape(SLOTS, LANES).astype(jnp.float32)
                total += v * v
        ssq_ref[...] = total

    for stage, ks in (
        (stage2, (0, 1, 7)), (stage3, (0,)), (stage2, (2, 6, 3, 5, 4)),
        (stage3, (1, 7)), (stage4, (0,)), (stage3, (2, 6, 3, 5)), (stage4, (1, 7)),
        (stage5, (0,)), (stage3, (4,)), (stage4, (2, 6)), (stage6, (0,)), (stage4, (3, 5)),
        (stage5, (1, 7)), (stage4, (4,)), (stage5, (2, 6)), (stage6, (1, 7)), (stage5, (3, 5)),
        (stage6, (2, 6)), (stage5, (4,)), (stage6, (3, 5, 4)),
    ):
        for k in ks:
            stage(k)

    for cp in small:
        cp.wait()
    for cp in w_copies:
        cp.wait()

    mean_square = jnp.sum(ssq_ref[...], axis=1, keepdims=True) * (1.0 / D)
    factor = lax.rsqrt(mean_square + EPS)
    acc_ref[...] = jnp.zeros_like(acc_ref)

    @pl.loop(0, NZ * 2)
    def _(i):
        z, h = i // 2, lax.rem(i, 2)
        parts = []
        for y in range(NY):
            v = g_ref[z, h, :, :, y].reshape(SLOTS, LANES).astype(jnp.float32)
            gain = gain_ref[pl.ds(z * 8 + y * 2 + h, 1), :]
            parts.append((v * factor * gain).astype(jnp.bfloat16))
        lhs = jnp.concatenate(parts, axis=1)
        rhs = w_ref[z, :, h].reshape(NY * LANES, COLS)
        acc_ref[...] += jnp.dot(lhs, rhs, preferred_element_type=jnp.float32)

    lane = lax.broadcasted_iota(jnp.int32, (SLOTS, LANES), 1)
    row = lax.broadcasted_iota(jnp.int32, (SLOTS, LANES), 0)
    slot = (((row >> 4) & 3) * 2 + (row >> 6)) * SG + (row & 15)
    choice = choice_ref[...]
    heat = jnp.zeros((1, LANES), jnp.float32)
    for n in range(16):
        heat = jnp.where(choice == n, heat_ref[n], heat)
    heat = jnp.sum(jnp.where(lane == slot, heat, 0.0), axis=1, keepdims=True)
    scaled = acc_ref[...] / heat

    offset = ((z0 * NY + y0) * (NX * NC) + x0 * NC + c0) * COLS
    top = jnp.max(scaled, axis=1, keepdims=True)
    total = jnp.sum(jnp.exp(scaled - top), axis=1, keepdims=True)
    top_row = jnp.sum(jnp.where(lane == row, top, 0.0), axis=0, keepdims=True)
    total_row = jnp.sum(jnp.where(lane == row, total, 0.0), axis=0, keepdims=True)
    stats = jnp.concatenate([top_row, total_row, jnp.zeros((6, LANES), jnp.float32)], axis=0)
    for c in range(NC):
        for x in range(NX):
            g = c * NX + x
            mine = scaled[g * SG : (g + 1) * SG]
            local = ids_ref[x, c] - offset
            cand = jnp.zeros((SG, LANES), jnp.float32)
            for t in range(COLS // LANES):
                at = local - t * LANES
                inside = (at >= 0) & (at < LANES)
                got = jnp.take_along_axis(
                    mine[:, t * LANES : (t + 1) * LANES], jnp.clip(at, 0, LANES - 1), axis=1,
                    mode="promise_in_bounds",
                )
                cand = jnp.where(inside, got, cand)
            m1_ref[c, x, :SG] = cand
            m1_ref[c, x, SG:] = stats

    for k in (2, 1, 3, 0):
        for kc in range(NC):
            if k or kc:
                cx, cc = xp(k), lax.rem(c0 + kc, NC)
                send(
                    m1_ref.at[cc, cx], r1_ref.at[c0, x0],
                    q1_send.at[k, kc], q1_recv.at[k, kc], {"x": cx, "c": cc},
                )
    r1_ref[c0, x0] = m1_ref[c0, x0]
    for k in (0, 1, 3, 2):
        for kc in range(NC):
            if k or kc:
                landed(
                    r1_ref.at[lax.rem(c0 + kc, NC), xp(NX - k)], q1_send.at[k, kc], q1_recv.at[k, kc]
                )

    def merged(parts):
        top = parts[0][SG : SG + 1]
        for p in parts[1:]:
            top = jnp.maximum(top, p[SG : SG + 1])
        total, cand = jnp.zeros_like(top), jnp.zeros((SG, LANES), jnp.float32)
        for p in parts:
            total += p[SG + 1 : SG + 2] * jnp.exp(p[SG : SG + 1] - top)
            cand += p[:SG]
        return cand, top, total

    def store(ref, value):
        cand, top, total = value
        ref[:SG] = cand
        ref[SG:] = jnp.concatenate([top, total, jnp.zeros((6, LANES), jnp.float32)], axis=0)

    store(m2_ref, merged([r1_ref[c, x] for c in range(NC) for x in range(NX)]))
    for k in (2, 1, 3):
        send(m2_ref, r2_ref.at[y0], q2_send.at[k], q2_recv.at[k], {"y": yp(k)})
    r2_ref[y0] = m2_ref[...]
    for k in (1, 3, 2):
        landed(r2_ref.at[yp(NY - k)], q2_send.at[k], q2_recv.at[k])

    store(m3_ref, merged([r2_ref[y] for y in range(NY)]))
    for k in reversed(ORDER[1:]):
        send(m3_ref, r3_ref.at[z0], q3_send.at[k], q3_recv.at[k], {"z": zp(k)})
    r3_ref[z0] = m3_ref[...]
    for k in ORDER[1:]:
        landed(r3_ref.at[zp(NZ - k)], q3_send.at[k], q3_recv.at[k])
    cand, top, total = merged([r3_ref[z] for z in range(NZ)])

    log_norm = top + jnp.log(total)
    lane16 = lax.broadcasted_iota(jnp.int32, (SG, LANES), 1)
    row16 = lax.broadcasted_iota(jnp.int32, (SG, LANES), 0)
    at_row = lane16 == (c0 * NX + x0) * SG + row16
    log_norm = jnp.sum(jnp.where(at_row, log_norm, 0.0), axis=1, keepdims=True)
    at_slot = lane16 == (x0 * NC + c0) * SG + row16
    keep = jnp.sum(jnp.where(at_slot, keep_ref[...], 0), axis=1, keepdims=True)
    kept = lane16 < keep
    kept_top = jnp.max(jnp.where(kept, cand, -3e38), axis=1, keepdims=True)
    kept_exp = jnp.where(kept, jnp.exp(jnp.where(kept, cand - kept_top, 0.0)), 0.0)
    kept_sum = jnp.sum(kept_exp, axis=1, keepdims=True)
    kept_mass = kept_top + jnp.log(kept_sum) - log_norm
    ren_out[...] = kept_exp / kept_sum
    stat_out[0:1] = jnp.sum(jnp.where(lane16 == row16, log_norm, 0.0), axis=0, keepdims=True)
    stat_out[1:2] = jnp.sum(jnp.where(lane16 == row16, kept_mass, 0.0), axis=0, keepdims=True)
    stat_out[2:8] = jnp.zeros((6, LANES), jnp.float32)

    for cp in sends:
        cp.wait_send()


def local(x, gain, w, heat, choice, ids, keep):
    x = x.reshape(SG, 2, LANES).transpose(1, 0, 2)
    w = w.reshape(NZ, NY, 2, LANES, COLS)
    gain = gain.astype(jnp.float32).reshape(D // LANES, LANES)
    ids = ids.reshape(NX, NC, SG, LANES)
    any_spec = pl.BlockSpec(memory_space=pl.ANY)
    vmem = pl.BlockSpec(memory_space=pltpu.VMEM)
    dma = pltpu.SemaphoreType.DMA
    f32, bf16 = jnp.float32, jnp.bfloat16
    stats, ren = pl.pallas_call(
        kernel,
        name="tail",
        out_shape=(
            jax.ShapeDtypeStruct((8, LANES), f32),
            jax.ShapeDtypeStruct((SG, LANES), f32),
        ),
        in_specs=[any_spec] * 4 + [pl.BlockSpec(memory_space=pltpu.SMEM)] + [any_spec] * 2,
        out_specs=(vmem, vmem),
        scratch_shapes=[
            pltpu.VMEM((NZ, 2, NC, NX, NY, SG, LANES), bf16),
            pltpu.VMEM((NZ, NY, 2, LANES, COLS), bf16),
            pltpu.VMEM((D // LANES, LANES), f32),
            pltpu.VMEM((NX, NC, SG, LANES), jnp.int32),
            pltpu.VMEM((1, LANES), jnp.int32),
            pltpu.VMEM((1, LANES), jnp.int32),
            pltpu.VMEM((SLOTS, LANES), f32),
            pltpu.VMEM((SLOTS, COLS), f32),
            pltpu.VMEM((NC, NX, SG + 8, LANES), f32),
            pltpu.VMEM((NC, NX, SG + 8, LANES), f32),
            pltpu.VMEM((NY, SG + 8, LANES), f32),
            pltpu.VMEM((NZ, SG + 8, LANES), f32),
            pltpu.VMEM((SG + 8, LANES), f32),
            pltpu.VMEM((SG + 8, LANES), f32),
            dma((5,)), dma((NZ,)),
            dma((NZ,)), dma((NZ,)),
            dma((NZ, NY)), dma((NZ, NY)), dma((NZ, NX)), dma((NZ, NX)),
            dma((NZ, NX)), dma((NZ, NX)), dma((NZ, NY)), dma((NZ, NY)),
            dma((NZ, NX)), dma((NZ, NX)), dma((NZ, NY)), dma((NZ, NY)),
            dma((NZ,)), dma((NZ,)),
            dma((NX, NC)), dma((NX, NC)), dma((NY,)), dma((NY,)), dma((NZ,)), dma((NZ,)),
        ],
        compiler_params=pltpu.CompilerParams(
            collective_id=0, has_side_effects=True, vmem_limit_bytes=40 * 1024 * 1024
        ),
    )(x, w, gain, ids, heat, choice.reshape(1, SLOTS), keep.reshape(1, SLOTS))
    return stats[0, :SG], stats[1, :SG], ren


def solution(mesh):
    torus = Mesh(mesh.devices.reshape(NZ, NY, NX, NC), ("z", "y", "x", "c"))
    zy, xc = ("z", "y"), ("x", "c")
    in_specs = (P(xc, zy), P(), P(None, (*zy, *xc)), P(), P(), P(), P())
    out_specs = (P(xc), P(xc), P(xc, None))
    return jax.shard_map(local, mesh=torus, in_specs=in_specs, out_specs=out_specs, check_vma=False)
```

time: 245 us -> 58.2 us (0.24)
  local copies, waits for them, and re-layouts: 133 us -> 8 us
  Pallas kernels: 0 us -> 48.6 us
  blocking collectives: 41.2 us -> 0 us
  waiting for transfers between devices: 37.6 us -> 0 us
  starting transfers between devices: 21.1 us -> 0 us
  other arithmetic: 6.33 us -> 0.72 us
  matrix products: 4.85 us -> 0 us
    gather x1 -> x0, local copies, waits for them, and re-layouts: 129 us -> none  [local(): jnp.take_along_axis(divided_scores, jnp.clip(local_ids, 0, col_count - 1)...]
    pallas_call x0 -> x1, Pallas kernels: none -> 48.6 us  [local(): pl.pallas_call(kernel, name='tail', out_shape=(jax.ShapeDtypeStruct((8, L...]
    all_to_all x2 -> x0, waiting for transfers between devices: 37.6 us -> none  [from_everyone(): return lax.all_to_all(copies, axis, split_axis=0, concat_axis=0, tiled=True)]
    all_gather x2 -> x0, blocking collectives: 32.6 us -> none  [gather_axes(): whole = lax.all_gather(whole, axes[number], axis=dim, tiled=True)]
    all_to_all x2 -> x0, starting transfers between devices: 21.1 us -> none  [from_everyone(): return lax.all_to_all(copies, axis, split_axis=0, concat_axis=0, tiled=True)]
    all_to_all x1 -> x0, blocking collectives: 8.59 us -> none  [side_by_side(): lax.all_to_all(both, axis, split_axis=split_dim, concat_axis=concat_dim,...]
    unnamed x5 -> x13, local copies, waits for them, and re-layouts: 0.02 us -> 7.48 us
    dot_general x1 -> x0, matrix products: 4.85 us -> none  [local(): jnp.dot(rows_normed(gather_directly(wide_rows, 'batch', 0), gain_full), o...]
  transfers between devices with their start and end apart: 2 -> 0, of which waited for: 2 -> 0; matrix products, arithmetic and copies ran while one was open for 1% -> 0% of each run, Pallas kernels for 0% -> 0%
where the time goes in v1:
time: 58.2 us; the launch traced here: 57.9 us
  Pallas kernels  48.6 us (84%)
  local copies, waits for them, and re-layouts  8 us (14%)
  other arithmetic  0.72 us (1%)
  between operations  0.65 us (1%)
    pallas_call x1, Pallas kernels, local(): pl.pallas_call(kernel, name='tail', out_shape=(jax.ShapeDtypeStruct((8, L...  48.6 us
    unnamed x13, local copies, waits for them, and re-layouts  7.48 us

profile of v1, /device:TPU:1, one launch (start us, length us, event | category | flops | bytes accessed | tf_op | source)
XLA Modules:
  0.0 57.9 jit_solution(17615317014905790543)
XLA Ops:
  0.6 0.0 copy-start
  0.6 0.7 %copy-done = bf16[16,256]{1,0:T(8,128)(2,1)S(1)} copy-done((bf16[16,256]{1,0:T(8,128)(2,1)S(1)}, bf16[16,256]{1,0:T(8,128)(2,1)}, u32[]{:S(2)}) %copy-start) | copy-done | bytes 8216
  1.3 0.7 %bitcast_convert_fusion.gain_hbm = f32[64,128]{1,0:T(8,128)S(1)} fusion(bf16[8192]{0:T(1024)(128)(2,1)} %param.8), kind=kLoop, calls=%fused_computation | loop fusion | flops 8192 | bytes 49152 | tf_op jit(solution)/shard_map/reshape | solution.py:284
  2.1 0.0 copy-start.1
  2.1 3.4 %copy-done.1 = bf16[8192,512]{1,0:T(8,128)(2,1)S(1)} copy-done((bf16[8192,512]{1,0:T(8,128)(2,1)S(1)}, bf16[8192,512]{1,0:T(8,128)(2,1)}, u32[]{:S(2)}) %copy-start.1) | copy-done | bytes 8388632
  5.4 0.0 copy-start.2
  5.4 0.8 %copy-done.2 = s32[128,128]{1,0:T(8,128)S(1)} copy-done((s32[128,128]{1,0:T(8,128)S(1)}, s32[128,128]{1,0:T(8,128)}, u32[]{:S(2)}) %copy-start.2) | copy-done | bytes 65560
  6.3 0.0 copy-start.3
  6.3 0.7 %copy-done.3 = f32[16]{0:T(128)S(1)} copy-done((f32[16]{0:T(128)S(1)}, f32[16]{0:T(128)}, u32[]{:S(2)}) %copy-start.3) | copy-done | bytes 88
  6.9 0.0 copy-start.4
  6.9 0.7 %copy-done.4 = s32[128]{0:T(128)S(1)} copy-done((s32[128]{0:T(128)S(1)}, s32[128]{0:T(128)}, u32[]{:S(2)}) %copy-start.4) | copy-done | bytes 536
  7.6 0.0 copy-start.5
  7.6 0.7 %copy-done.5 = s32[128]{0:T(128)S(1)} copy-done((s32[128]{0:T(128)S(1)}, s32[128]{0:T(128)}, u32[]{:S(2)}) %copy-start.5) | copy-done | bytes 536
  8.2 48.6 %tail.1 = (f32[8,128]{1,0:T(8,128)S(1)}, f32[16,128]{1,0:T(8,128)S(1)}) custom-call(bf16[2,16,128]{2,1,0:T(8,128)(2,1)S(1)} %bitcast_bitcast_fusion.x_hbm, bf16[8,4,2,128,512]{4,3,2,1,0:T(8,128)(2,1)S(1)} %bitcast.18, f32[64,128]{1,0:T(8,128)S(1)} %bitcast_convert_fusion.gain_hbm, s32[4,2,16,128]{3,2,1,0:T(8,128)S(1)} %bitcast.19, f32[16]{0:T(128)S(1)} %copy-done.3, ...), custom_call_target="tpu_custom_call" | custom-call | tf_op jit(solution)/shard_map/tail/pallas_call | solution.py:290
  56.8 0.5 slice_bitcast_fusion
  57.3 0.6 %copy.14 = f32[16,128]{1,0:T(8,128)} copy(f32[16,128]{1,0:T(8,128)S(1)} %get-tuple-element.14) | data formatting | bytes 16384
  (1 shorter events, 0.0 us)
Async XLA Ops:
  0.6 0.7 %copy-start = (bf16[16,256]{1,0:T(8,128)(2,1)S(1)}, bf16[16,256]{1,0:T(8,128)(2,1)}, u32[]{:S(2)}) copy-start(bf16[16,256]{1,0:T(8,128)(2,1)} %param.7) | copy-start | bytes 24580
  2.1 3.4 %copy-start.1 = (bf16[8192,512]{1,0:T(8,128)(2,1)S(1)}, bf16[8192,512]{1,0:T(8,128)(2,1)}, u32[]{:S(2)}) copy-start(bf16[8192,512]{1,0:T(8,128)(2,1)} %param.9) | copy-start | bytes 25165828
  5.4 0.8 %copy-start.2 = (s32[128,128]{1,0:T(8,128)S(1)}, s32[128,128]{1,0:T(8,128)}, u32[]{:S(2)}) copy-start(s32[128,128]{1,0:T(8,128)} %param.12) | copy-start | bytes 196612
  6.3 0.7 %copy-start.3 = (f32[16]{0:T(128)S(1)}, f32[16]{0:T(128)}, u32[]{:S(2)}) copy-start(f32[16]{0:T(128)} %heat_ref.1) | copy-start | bytes 196
  6.9 0.7 %copy-start.4 = (s32[128]{0:T(128)S(1)}, s32[128]{0:T(128)}, u32[]{:S(2)}) copy-start(s32[128]{0:T(128)} %param.11) | copy-start | bytes 1540
  7.6 0.7 %copy-start.5 = (s32[128]{0:T(128)S(1)}, s32[128]{0:T(128)}, u32[]{:S(2)}) copy-start(s32[128]{0:T(128)} %param.13) | copy-start | bytes 1540

commit v2 on v1

v2 whole, which is shorter than its diff:
```python
import jax
import jax.numpy as jnp
from jax import lax
from jax.experimental import pallas as pl
from jax.experimental.pallas import tpu as pltpu
from jax.sharding import Mesh
from jax.sharding import PartitionSpec as P

NZ, NY, NX, NC = 8, 4, 4, 2
SG = 16
ROWS = SG + 2
COLS = 512
LANES = 128
SLOTS = 128
D = 8192
EPS = 1e-06
MESH_ID = pl.DeviceIdType.MESH


GROUPS = ((0, 1, 1), (1, 6, 2), (2, 4, 2), (3, 1, 3))
KIB_ROWS = 2


def offsets(g):
    first, stride, count = GROUPS[g]
    return [first + stride * n for n in range(count)]


def kernel(
    x_hbm, w_hbm, gain_hbm, ids_hbm, heat_hbm, choice_hbm, keep_hbm,
    out_ref,
    g_ref, w_ref, gain_ref, ids_ref, heat_ref, choice_ref, keep_ref,
    wide_ref, ssq_ref, acc_ref, m1_ref, r1_ref, r2_ref, r3_ref, m2_ref, m3_ref, size_ref,
    in_sem, w_sem, s1, s2, s3, s4, q_recv, ag_send, q_send,
):
    z0, y0, x0, c0 = (lax.axis_index(a) for a in ("z", "y", "x", "c"))

    def zp(k):
        return lax.rem(z0 + k, NZ)

    def yp(k):
        return lax.rem(y0 + k, NY)

    def xp(k):
        return lax.rem(x0 + k, NX)

    def cp_(k):
        return lax.rem(c0 + k, NC)

    for h in range(2):
        pltpu.make_async_copy(
            x_hbm.at[:, pl.ds(h * LANES, LANES)], g_ref.at[z0, h, c0, x0, y0], in_sem.at[0]
        ).start()

    peers = [{"z": zp(k)} for k in range(1, NZ)] + [{"y": yp(k)} for k in range(1, NY)]
    peers += [{"x": xp(k), "c": cp_(kc)} for k in range(NX) for kc in range(NC) if k or kc]
    barrier = pltpu.get_barrier_semaphore()
    for peer in peers:
        pl.semaphore_signal(barrier, inc=1, device_id=peer, device_id_type=MESH_ID)

    for z in range(NZ):
        pltpu.make_async_copy(w_hbm.at[z], w_ref.at[z], w_sem).start()
    small = []
    for n, (src, dst) in enumerate(
        (
            (gain_hbm, gain_ref), (ids_hbm, ids_ref), (heat_hbm, heat_ref),
            (choice_hbm, choice_ref), (keep_hbm, keep_ref),
        )
    ):
        cp = pltpu.make_async_copy(src, dst, in_sem.at[1 + n])
        cp.start()
        small.append(cp)
    own = g_ref.at[z0, :, c0, x0, y0]
    pltpu.make_async_copy(own, own, in_sem.at[0]).wait()
    pl.semaphore_wait(barrier, len(peers))

    sent = {}

    def send(src, dst, ssem, rsem, to, kib):
        pltpu.make_async_remote_copy(
            src_ref=src, dst_ref=dst, send_sem=ssem, recv_sem=rsem, device_id=to, device_id_type=MESH_ID
        ).start()
        sent[id(ssem)] = sent.get(id(ssem), 0) + kib

    def drain(sem, kib):
        whole = size_ref.at[pl.ds(0, kib * KIB_ROWS)]
        pltpu.make_async_copy(whole, whole, sem).wait()

    for g in reversed(range(1, len(GROUPS))):
        for k in offsets(g):
            send(own, own, ag_send, s1.at[g], {"z": zp(k)}, 8)

    def stage2(g):
        if g:
            drain(s1.at[g], 8 * GROUPS[g][2])
        for k in offsets(g):
            z = zp(NZ - k)
            for d in (2, 1, 3):
                a = g_ref.at[z, 0, c0, x0, y0]
                send(a, a, ag_send, s2.at[g], {"y": yp(d)}, 4)
                b = g_ref.at[z, 1, c0, x0, y0]
                send(b, b, ag_send, s2.at[g], {"x": xp(d)}, 4)

    def stage3(g):
        drain(s2.at[g], 24 * GROUPS[g][2])
        for k in offsets(g):
            z = zp(NZ - k)
            for d in (2, 1, 3):
                a = g_ref.at[z, 0, c0, x0]
                send(a, a, ag_send, s3.at[g], {"x": xp(d)}, 16)
                b = g_ref.at[z, 1, c0, :, y0]
                send(b, b, ag_send, s3.at[g], {"y": yp(d)}, 16)

    def stage4(g):
        drain(s3.at[g], 96 * GROUPS[g][2])
        for k in offsets(g):
            blk = g_ref.at[zp(NZ - k), :, c0]
            send(blk, blk, ag_send, s4.at[g], {"c": cp_(1)}, 128)

    def compute(g):
        if g == 0:
            for cp in small:
                cp.wait()
            pltpu.make_async_copy(w_ref, w_ref, w_sem).wait()
            wide_ref[...] = gain_ref[...].astype(jnp.float32)
            ssq_ref[...] = jnp.zeros_like(ssq_ref)
            acc_ref[...] = jnp.zeros_like(acc_ref)
        drain(s4.at[g], 128 * GROUPS[g][2])
        first, stride, count = GROUPS[g]

        def chunk(n):
            z = lax.rem(z0 + (NZ - first) + (NZ - stride) * n, NZ)
            high, low = [], []
            total = ssq_ref[...]
            for y in range(NY):
                for h in range(2):
                    v = g_ref[z, h, :, :, y].reshape(SLOTS, LANES).astype(jnp.float32)
                    total += v * v
                    p = v * wide_ref[pl.ds(z * 8 + y * 2 + h, 1), :]
                    hi = p.astype(jnp.bfloat16)
                    high.append(hi)
                    low.append((p - hi.astype(jnp.float32)).astype(jnp.bfloat16))
            ssq_ref[...] = total
            lhs = jnp.concatenate([jnp.concatenate(high, axis=1), jnp.concatenate(low, axis=1)], axis=0)
            rhs = w_ref[z].reshape(2 * NY * LANES, COLS)
            both = jnp.dot(lhs, rhs, preferred_element_type=jnp.float32)
            acc_ref[...] += both[:SLOTS] + both[SLOTS:]

        if count == 1:
            chunk(0)
        else:
            pl.loop(0, count)(chunk)

    stage2(0)
    stage2(1)
    stage2(2)
    stage3(0)
    stage2(3)
    stage3(1)
    stage3(2)
    stage4(0)
    stage3(3)
    compute(0)
    stage4(1)
    stage4(2)
    compute(1)
    stage4(3)
    compute(2)
    compute(3)

    mean_square = jnp.sum(ssq_ref[...], axis=1, keepdims=True) * (1.0 / D)
    factor = lax.rsqrt(mean_square + EPS)

    lane = lax.broadcasted_iota(jnp.int32, (SLOTS, LANES), 1)
    row = lax.broadcasted_iota(jnp.int32, (SLOTS, LANES), 0)
    slot = (((row >> 4) & 3) * 2 + (row >> 6)) * SG + (row & 15)
    choice = choice_ref[...]
    heat = jnp.zeros((1, LANES), jnp.float32)
    for n in range(16):
        heat = jnp.where(choice == n, heat_ref[n], heat)
    heat = jnp.sum(jnp.where(lane == slot, heat, 0.0), axis=1, keepdims=True)
    scaled = acc_ref[...] * (factor / heat)

    offset = ((z0 * NY + y0) * (NX * NC) + x0 * NC + c0) * COLS
    top = jnp.max(scaled, axis=1, keepdims=True)
    total = jnp.sum(jnp.exp(scaled - top), axis=1, keepdims=True)
    top_row = jnp.sum(jnp.where(lane == row, top, 0.0), axis=0, keepdims=True)
    total_row = jnp.sum(jnp.where(lane == row, total, 0.0), axis=0, keepdims=True)
    stats = jnp.concatenate([top_row, total_row], axis=0)
    for c in range(NC):
        for x in range(NX):
            g = c * NX + x
            mine = scaled[g * SG : (g + 1) * SG]
            local = ids_ref[x, c] - offset
            cand = jnp.zeros((SG, LANES), jnp.float32)
            for t in range(COLS // LANES):
                at = local - t * LANES
                inside = (at >= 0) & (at < LANES)
                got = jnp.take_along_axis(
                    mine[:, t * LANES : (t + 1) * LANES], jnp.clip(at, 0, LANES - 1), axis=1,
                    mode="promise_in_bounds",
                )
                cand = jnp.where(inside, got, cand)
            m1_ref[c, x, :SG] = cand
            m1_ref[c, x, SG:ROWS] = stats

    part = pl.ds(0, ROWS)
    for k in (2, 1, 3, 0):
        for kc in range(NC):
            if k or kc:
                cx, cc = xp(k), cp_(kc)
                send(
                    m1_ref.at[cc, cx, part], r1_ref.at[c0, x0, part],
                    q_send, q_recv.at[0], {"x": cx, "c": cc}, 9,
                )
    r1_ref[c0, x0, :ROWS] = m1_ref[c0, x0, :ROWS]
    drain(q_recv.at[0], 7 * 9)

    def merged(parts):
        top = parts[0][SG : SG + 1]
        for p in parts[1:]:
            top = jnp.maximum(top, p[SG : SG + 1])
        total, cand = jnp.zeros_like(top), jnp.zeros((SG, LANES), jnp.float32)
        for p in parts:
            total += p[SG + 1 : SG + 2] * jnp.exp(p[SG : SG + 1] - top)
            cand += p[:SG]
        return cand, top, total

    def store(ref, value):
        cand, top, total = value
        ref[:SG] = cand
        ref[SG:ROWS] = jnp.concatenate([top, total], axis=0)

    store(m2_ref, merged([r1_ref[c, x, :ROWS] for c in range(NC) for x in range(NX)]))
    for k in (2, 1, 3):
        send(m2_ref.at[part], r2_ref.at[y0, part], q_send, q_recv.at[1], {"y": yp(k)}, 9)
    r2_ref[y0, :ROWS] = m2_ref[:ROWS]
    drain(q_recv.at[1], 3 * 9)

    store(m3_ref, merged([r2_ref[y, :ROWS] for y in range(NY)]))
    for k in (4, 3, 5, 2, 6, 1, 7):
        send(m3_ref.at[part], r3_ref.at[z0, part], q_send, q_recv.at[2], {"z": zp(k)}, 9)
    r3_ref[z0, :ROWS] = m3_ref[:ROWS]
    drain(q_recv.at[2], 7 * 9)
    cand, top, total = merged([r3_ref[z, :ROWS] for z in range(NZ)])

    log_norm = top + jnp.log(total)
    lane16 = lax.broadcasted_iota(jnp.int32, (SG, LANES), 1)
    row16 = lax.broadcasted_iota(jnp.int32, (SG, LANES), 0)
    at_row = lane16 == (c0 * NX + x0) * SG + row16
    log_norm = jnp.sum(jnp.where(at_row, log_norm, 0.0), axis=1, keepdims=True)
    at_slot = lane16 == (x0 * NC + c0) * SG + row16
    keep = jnp.sum(jnp.where(at_slot, keep_ref[...], 0), axis=1, keepdims=True)
    kept = lane16 < keep
    kept_top = jnp.max(jnp.where(kept, cand, -3e38), axis=1, keepdims=True)
    kept_exp = jnp.where(kept, jnp.exp(jnp.where(kept, cand - kept_top, 0.0)), 0.0)
    kept_sum = jnp.sum(kept_exp, axis=1, keepdims=True)
    kept_mass = kept_top + jnp.log(kept_sum) - log_norm
    out_ref[8:] = kept_exp / kept_sum
    out_ref[0:1] = jnp.sum(jnp.where(lane16 == row16, log_norm, 0.0), axis=0, keepdims=True)
    out_ref[1:2] = jnp.sum(jnp.where(lane16 == row16, kept_mass, 0.0), axis=0, keepdims=True)
    out_ref[2:8] = jnp.zeros((6, LANES), jnp.float32)

    drain(ag_send, sent[id(ag_send)])
    drain(q_send, sent[id(q_send)])


def local(x, gain, w, heat, choice, ids, keep):
    w = w.reshape(NZ, NY, 2, LANES, COLS)
    gain = gain.reshape(D // LANES, LANES)
    ids = ids.reshape(NX, NC, SG, LANES)
    hbm = pl.BlockSpec(memory_space=pl.ANY)
    vmem = pl.BlockSpec(memory_space=pltpu.VMEM)
    operands = (x, w, gain, ids, heat, choice.reshape(1, SLOTS), keep.reshape(1, SLOTS))
    dma = pltpu.SemaphoreType.DMA
    f32, bf16 = jnp.float32, jnp.bfloat16
    out = pl.pallas_call(
        kernel,
        name="tail",
        out_shape=jax.ShapeDtypeStruct((8 + SG, LANES), f32),
        in_specs=[hbm] * 7,
        out_specs=vmem,
        scratch_shapes=[
            pltpu.VMEM((NZ, 2, NC, NX, NY, SG, LANES), bf16),
            pltpu.VMEM((NZ, NY, 2, LANES, COLS), bf16),
            pltpu.VMEM((D // LANES, LANES), bf16),
            pltpu.VMEM((NX, NC, SG, LANES), jnp.int32),
            pltpu.SMEM((16,), f32),
            pltpu.VMEM((1, LANES), jnp.int32),
            pltpu.VMEM((1, LANES), jnp.int32),
            pltpu.VMEM((D // LANES, LANES), f32),
            pltpu.VMEM((SLOTS, LANES), f32),
            pltpu.VMEM((SLOTS, COLS), f32),
            pltpu.VMEM((NC, NX, SG + 8, LANES), f32),
            pltpu.VMEM((NC, NX, SG + 8, LANES), f32),
            pltpu.VMEM((NY, SG + 8, LANES), f32),
            pltpu.VMEM((NZ, SG + 8, LANES), f32),
            pltpu.VMEM((SG + 8, LANES), f32),
            pltpu.VMEM((SG + 8, LANES), f32),
            pltpu.VMEM((4096, LANES), f32),
            dma((6,)), dma, dma((4,)), dma((4,)), dma((4,)), dma((4,)), dma((3,)), dma, dma,
        ],
        compiler_params=pltpu.CompilerParams(
            collective_id=0, has_side_effects=True, vmem_limit_bytes=32 * 1024 * 1024
        ),
    )(*(pltpu.with_memory_space_constraint(a, pltpu.HBM) for a in operands))
    return out[0, :SG], out[1, :SG], out[8:]


def solution(mesh):
    torus = Mesh(mesh.devices.reshape(NZ, NY, NX, NC), ("z", "y", "x", "c"))
    zy, xc = ("z", "y"), ("x", "c")
    in_specs = (P(xc, zy), P(), P(None, (*zy, *xc)), P(), P(), P(), P())
    out_specs = (P(xc), P(xc), P(xc, None))
    return jax.shard_map(local, mesh=torus, in_specs=in_specs, out_specs=out_specs, check_vma=False)
```

time: 58.2 us -> 39.3 us (0.68)
  Pallas kernels: 48.6 us -> 37.4 us
  local copies, waits for them, and re-layouts: 8 us -> 1.12 us
  other arithmetic: 0.72 us -> 0 us
    pallas_call x1, Pallas kernels: 48.6 us -> 37.4 us  [local(): pl.pallas_call(kernel, name='tail', out_shape=jax.ShapeDtypeStruct((8 + S...]
    unnamed x13 -> x0, local copies, waits for them, and re-layouts: 7.48 us -> none
    reshape x1 -> x0, other arithmetic: 0.72 us -> none  [local(): gain = gain.astype(jnp.float32).reshape(D // LANES, LANES)]
    slice x0 -> x1, local copies, waits for them, and re-layouts: none -> 0.6 us  [local(): return (out[0, :SG], out[1, :SG], out[8:])]
where the time goes in v2:
time: 39.3 us; the launch traced here: 39.2 us
  Pallas kernels  37.4 us (95%)
  local copies, waits for them, and re-layouts  1.12 us (3%)
  between operations  0.64 us (2%)
    pallas_call x1, Pallas kernels, local(): pl.pallas_call(kernel, name='tail', out_shape=jax.ShapeDtypeStruct((8 + S...  37.4 us

profile of v2, /device:TPU:1, one launch (start us, length us, event | category | flops | bytes accessed | tf_op | source)
XLA Modules:
  0.0 39.2 jit_solution(9732437609913058969)
XLA Ops:
  0.6 37.4 %tail.1 = f32[24,128]{1,0:T(8,128)S(1)} custom-call(bf16[16,256]{1,0:T(8,128)(2,1)} %x_hbm.1, bf16[8,4,2,128,512]{4,3,2,1,0:T(8,128)(2,1)} %bitcast.9, bf16[64,128]{1,0:T(8,128)(2,1)} %bitcast.11, s32[4,2,16,128]{3,2,1,0:T(8,128)} %bitcast.10, f32[16]{0:T(128)} %heat_hbm.1, s32[1,128]{1,0:T(1,128)} %bitcast.12, s32[1,128]{1,0:T(1,128)} %bitcast.13), custom_call_target="tpu_custom_call" | custom-call | tf_op jit(solution)/shard_map/tail/pallas_call | solution.py:277
  38.1 0.5 %slice_bitcast_fusion = (f32[16]{0:T(128)}, f32[16]{0:T(128)}) fusion(f32[24,128]{1,0:T(8,128)S(1)} %tail.1), kind=kLoop, calls=%fused_computation | loop fusion | bytes 256 | tf_op jit(solution)/shard_map/squeeze | solution.py:307
  38.6 0.6 %slice.11 = f32[16,128]{1,0:T(8,128)} slice(f32[24,128]{1,0:T(8,128)S(1)} %tail.1), slice={[8:24], [0:128]} | slice | bytes 16384 | tf_op jit(solution)/shard_map/slice | solution.py:307
